TPU v7x, 32 devices: a whole 2x2x4 slice. The times are simulated.
32 devices in a mesh: rows: 8 (over z, y), cols: 4 (over x, core).
Axes of the slice: x: 2, y: 2, z: 4, core: 2. Of those that a mesh axis runs over, the one named last changes fastest.
Arguments:
- tile_values: bfloat16 [8, 4, 320, 128, 128], P('rows', 'cols'), may hold values from -0.0625 to 0.0625
- tile_rows: int32 [8, 4, 320], P('rows', 'cols'), may hold values from 0 to 7
- tile_cols: int32 [8, 4, 320], P('rows', 'cols'), may hold values from 0 to 15
- tile_counts: int32 [8, 4], P('rows', 'cols'), may hold values from 1 to 320, as said below
- sketch: bfloat16 [8192, 160], P(('rows', 'cols')), may hold values from -6 to 6
Outputs:
- basis: float32 [8192, 160], P(('rows', 'cols'))
- factor: float32 [160, 160], replicated
Inputs may be any that keep to these rules, and one draw needn't show every extreme that they name: Only the first tile_counts[r, c] slots of list (r, c) are live; some list has all 320 slots live in every draw. `tile_cols`: the same place may stand in several live slots of a list.
All inputs are finite; a program needn't handle non-finite values.
Results may differ from a plain program's by a relative error of at most 0.0029.
Values may be sent and summed in bfloat16 or wider, within the bound.
A program may use at most 128 MiB of HBM per device.

v0:
```python
import math
import jax
import jax.numpy as jnp
from jax import lax
from jax.sharding import PartitionSpec as P

POWER = 2
RT = 8


def accumulate(block_list, row_list, col_list, live_count, gathered, height):
    slot_total = block_list.shape[0]
    tile_size = block_list.shape[1]
    sketch_width = gathered.shape[1]
    tile_stack = gathered.reshape(-1, tile_size, sketch_width)
    block_size = math.gcd(32, slot_total)

    def one_block(block_index, running):
        first_slot = block_index * block_size
        block_values = lax.dynamic_slice_in_dim(block_list, first_slot, block_size, 0)
        rowids = lax.dynamic_slice_in_dim(row_list, first_slot, block_size, 0)
        colids = lax.dynamic_slice_in_dim(col_list, first_slot, block_size, 0)
        picked = jnp.take(tile_stack, colids, axis=0)
        products = jnp.einsum(
            "sab,sbk->sak", block_values, picked, preferred_element_type=jnp.float32
        )
        live_mask = (first_slot + jnp.arange(block_size, dtype=jnp.int32) < live_count).astype(
            jnp.float32
        )
        return running.at[rowids].add(products * live_mask[:, None, None])

    block_count = (live_count + block_size - 1) // block_size
    initial = jnp.zeros((height, tile_size, sketch_width), jnp.float32)
    running = lax.fori_loop(0, block_count, one_block, initial)
    return running.reshape(height * tile_size, sketch_width)


def shards(tile_values, tile_rows, tile_cols, tile_counts, sketch):
    own_values = tile_values[0, 0]
    own_rows = tile_rows[0, 0]
    own_cols = tile_cols[0, 0]
    own_count = tile_counts[0, 0]
    nodes_total = sketch.shape[0] * lax.axis_size("rows") * lax.axis_size("cols")
    current = sketch
    solved = None
    factor = None
    for power in range(POWER):
        gathered = lax.all_gather(current, "rows", axis=0, tiled=True)
        partial_value = accumulate(own_values, own_rows, own_cols, own_count, gathered, RT)
        whole = lax.psum(partial_value, "cols")
        gram_matrix = lax.psum(jnp.dot(whole.T, whole, precision=lax.Precision.HIGHEST), "rows")
        share_rows = whole.shape[0] // lax.axis_size("cols")
        owned = lax.dynamic_slice_in_dim(whole, lax.axis_index("cols") * share_rows, share_rows, 0)
        gram_matrix = gram_matrix / nodes_total
        factor = jnp.linalg.cholesky(gram_matrix)
        solved = lax.linalg.triangular_solve(
            factor, owned, left_side=False, lower=True, transpose_a=True
        )
        current = solved.astype(jnp.bfloat16)
    return (solved, factor)


def solution(mesh):
    placed = (
        P("rows", "cols", None, None, None),
        P("rows", "cols", None),
        P("rows", "cols", None),
        P("rows", "cols"),
        P(("rows", "cols"), None),
    )
    return jax.shard_map(
        shards,
        mesh=mesh,
        in_specs=placed,
        out_specs=(P(("rows", "cols"), None), P()),
        check_vma=False,
    )
```

profile of v0, /device:TPU:0, one launch (start us, length us, event | category | flops | bytes accessed | tf_op | source)
XLA Modules:
  0.0 597.8 jit_solution(8288383398452547619)
XLA Ops:
  7.9 0.7 reduce.8
  8.6 0.7 reduce.9
  9.3 33.6 %all_gather.6 = bf16[2048,160]{0,1:T(8,128)(2,1)S(1)} all-gather(bf16[256,160]{0,1:T(8,128)(2,1)} %param.18), channel_id=1, replica_groups=mesh['rows'=8,'cols'=4] {'rows'}, dimensions={0}, use_global_device_ids=true | all-gather | bytes 737280 | tf_op jit(solution)/shard_map/all_gather | solution.py:48
  42.9 1.3 copy.17
  44.2 19.8 %while.23 = (s32[]{:T(128)}, f32[8,128,160]{1,2,0:T(8,128)S(1)}, s32[]{:T(128)}, s32[320]{0:T(512)S(1)}, bf16[320,128,128]{2,1,0:T(8,128)(2,1)}, /*index=5*/s32[...) while((s32[]{:T(128)}, f32[8,128,160]{1,2,0:T(8,128)S(1)}, ...), condition=%wide.region_2.4_spmd, body=%wide.region_0.3_spmd.sunk | while | flops 169739648 | bytes 16258423 | solution.py:34
  44.3 0.7 compare_and_fusion.4
  45.0 3.3 gather_fusion
  48.3 2.8 fusion.69
  51.1 3.0 scatter_fusion
  54.1 0.7 compare_and_fusion.4
  54.9 3.3 gather_fusion
  58.1 2.8 fusion.69
  61.0 3.0 scatter_fusion
  64.0 0.9 copy_bitcast_fusion.1
  65.0 110.6 %all-reduce.8.cloned.1.call-done = f32[1024,160]{0,1:T(8,128)} async-done(((f32[1024,160]{0,1:T(8,128)}), f32[1024,160]{0,1:T(8,128)}) %all-reduce.8.cloned.1.call-update) | async-done | bytes 655376 | tf_op jit(solution)/shard_map/psum | solution.py:50
  175.6 2.6 fusion.45
  178.6 71.0 %all-reduce.10.cloned.1.call-done = f32[160,160]{0,1:T(8,128)} async-done(((f32[160,160]{0,1:T(8,128)}), f32[160,160]{0,1:T(8,128)}) %all-reduce.10.cloned.1.call-update) | async-done | bytes 102416 | tf_op jit(solution)/shard_map/psum | solution.py:51
  249.6 0.9 broadcast_multiply_fusion.1
  250.6 0.9 fusion.21
  251.6 11.7 %cholesky.136 = f32[128,128]{1,0:T(8,128)S(1)} custom-call(f32[128,128]{1,0:T(8,128)S(1)} %cholesky.208), custom_call_target="Cholesky" | custom-call | tf_op jit(solution)/shard_map/jit(cholesky)/cholesky | solution.py:55
  263.4 9.8 %custom-call.13 = f32[1,128,128]{1,2,0:T(8,128)S(1)} custom-call(f32[1,128,128]{2,1,0:T(8,128)S(1)} %get-tuple-element.178), custom_call_target="InvertDiagBlocksLowerTriangular" | custom-call | tf_op jit(solution)/shard_map/jit(cholesky)/cholesky | solution.py:55
  273.5 2.9 cholesky.156
  279.2 19.7 %custom-call.14 = f32[2,128,128]{1,2,0:T(8,128)S(1)} custom-call(f32[2,128,128]{2,1,0:T(8,128)S(1)} %pad_maximum_fusion.1), custom_call_target="InvertDiagBlocksLowerTriangular" | custom-call | tf_op jit(solution)/shard_map/triangular_solve/custom-call.0 | solution.py:56
  298.8 1.2 fusion.26
  300.1 1.0 convolution_subtract_fusion.1
  301.3 32.0 %all_gather.7 = bf16[2048,160]{0,1:T(8,128)(2,1)S(1)} all-gather(bf16[256,160]{0,1:T(8,128)(2,1)S(1)} %maximum_convert_fusion), channel_id=1, replica_groups=mesh['rows'=8,'cols'=4] {'rows'}, dimensions={0}, use_global_device_ids=true | all-gather | bytes 737280 | tf_op jit(solution)/shard_map/all_gather | solution.py:48
  333.3 1.3 copy.29
  334.7 19.8 %while.24 = (s32[]{:T(128)}, f32[8,128,160]{1,2,0:T(8,128)S(1)}, s32[]{:T(128)}, s32[320]{0:T(512)S(1)}, bf16[320,128,128]{2,1,0:T(8,128)(2,1)}, /*index=5*/s32[...) while((s32[]{:T(128)}, f32[8,128,160]{1,2,0:T(8,128)S(1)}, ...), condition=%wide.region_11.15_spmd, body=%wide.region_9.14_spmd.sunk | while | flops 169739648 | bytes 16258423 | solution.py:34
  334.7 0.7 compare_and_fusion.5
  335.4 3.3 gather_fusion.1
  338.7 2.8 fusion.72
  341.6 3.0 scatter_fusion.1
  344.6 0.7 compare_and_fusion.5
  345.3 3.3 gather_fusion.1
  348.6 2.8 fusion.72
  351.5 3.0 scatter_fusion.1
  354.5 0.9 copy_bitcast_fusion
  355.7 108.8 %all-reduce.12.cloned.1.call-done = f32[1024,160]{0,1:T(8,128)} async-done(((f32[1024,160]{0,1:T(8,128)}), f32[1024,160]{0,1:T(8,128)}) %all-reduce.12.cloned.1.call-update) | async-done | bytes 655376 | tf_op jit(solution)/shard_map/psum | solution.py:50
  464.4 2.6 fusion.46
  467.1 71.1 %all-reduce.14.cloned.1.call-done = f32[160,160]{0,1:T(8,128)} async-done(((f32[160,160]{0,1:T(8,128)}), f32[160,160]{0,1:T(8,128)}) %all-reduce.14.cloned.1.call-update) | async-done | bytes 102416 | tf_op jit(solution)/shard_map/psum | solution.py:51
  538.3 0.9 broadcast_multiply_fusion
  539.3 0.9 fusion.20
  540.3 11.7 %cholesky.174 = f32[128,128]{1,0:T(8,128)S(1)} custom-call(f32[128,128]{1,0:T(8,128)S(1)} %cholesky.211), custom_call_target="Cholesky" | custom-call | tf_op jit(solution)/shard_map/jit(cholesky)/cholesky | solution.py:55
  552.0 9.8 %custom-call.15 = f32[1,128,128]{1,2,0:T(8,128)S(1)} custom-call(f32[1,128,128]{2,1,0:T(8,128)S(1)} %get-tuple-element.176), custom_call_target="InvertDiagBlocksLowerTriangular" | custom-call | tf_op jit(solution)/shard_map/jit(cholesky)/cholesky | solution.py:55
  562.2 2.9 cholesky.194
  568.5 19.7 %custom-call.16 = f32[2,128,128]{1,2,0:T(8,128)S(1)} custom-call(f32[2,128,128]{2,1,0:T(8,128)S(1)} %pad_maximum_fusion.2), custom_call_target="InvertDiagBlocksLowerTriangular" | custom-call | tf_op jit(solution)/shard_map/triangular_solve/custom-call.0 | solution.py:56
  588.2 1.2 fusion.24
  589.4 1.0 convolution_subtract_fusion
  (51 shorter events, 6.7 us)
Async XLA Ops:
  7.2 168.5 %all-reduce.8.cloned.1.call-start = ((), (), s32[]{:S(2)}) async-start(), calls=%async_computation | async-start | bytes 1310720 | tf_op jit(solution)/shard_map/psum | solution.py:50
  65.0 184.6 %all-reduce.10.cloned.1.call-start = ((), (), s32[]{:S(2)}) async-start(), calls=%async_computation.1 | async-start | bytes 327680 | tf_op jit(solution)/shard_map/psum | solution.py:51
  178.3 286.1 %all-reduce.12.cloned.1.call-start = ((), (), s32[]{:S(2)}) async-start(), calls=%async_computation.2 | async-start | bytes 1310720 | tf_op jit(solution)/shard_map/psum | solution.py:50
  355.4 182.8 %all-reduce.14.cloned.1.call-start = ((), (), s32[]{:S(2)}) async-start(), calls=%async_computation.3 | async-start | bytes 327680 | tf_op jit(solution)/shard_map/psum | solution.py:51
Sparse Core Ops, SparseCore 0:
  65.1 110.4 all-reduce.7
  179.5 70.0 all-reduce.9
  355.5 108.8 all-reduce.11
  468.2 70.0 all-reduce.13
where the time goes:
time: 600 us; the launch traced here: 598 us
  waiting for transfers between devices  362 us (60%)
  other arithmetic  113 us (19%)
  blocking collectives  65.7 us (11%)
  matrix products  21.9 us (4%)
  local copies, waits for them, and re-layouts  17.8 us (3%)
  between operations  17.3 us (3%)
    psum x2, waiting for transfers between devices, shards(): whole = lax.psum(partial_value, 'cols')  219 us
    psum x2, waiting for transfers between devices, shards(): lax.psum(jnp.dot(whole.T, whole, precision=lax.Precision.HIGHEST), 'rows')  142 us
    all_gather x2, blocking collectives, shards(): gathered = lax.all_gather(current, 'rows', axis=0, tiled=True)  65.7 us
    another operation x14, other arithmetic, shards(): factor = jnp.linalg.cholesky(gram_matrix)  51.6 us
    another operation x11, other arithmetic, shards(): lax.linalg.triangular_solve(factor, owned, left_side=False, lower=True, t...  40.9 us
    gather x4, local copies, waits for them, and re-layouts, one_block(): picked = jnp.take(tile_stack, colids, axis=0)  13 us
  transfers between devices with their start and end apart: 4, of which 4 were waited for; matrix products, arithmetic and copies ran while one was open for 0% of the time, Pallas kernels for 0%

commit v1 on v0

--- a/solution.py
+++ b/solution.py
@@ -47,7 +47,8 @@
     for power in range(POWER):
         gathered = lax.all_gather(current, "rows", axis=0, tiled=True)
         partial_value = accumulate(own_values, own_rows, own_cols, own_count, gathered, RT)
-        whole = lax.psum(partial_value, "cols")
+        blocks = lax.all_gather(partial_value, "cols")
+        whole = jnp.sum(blocks, axis=0)
         gram_matrix = lax.psum(jnp.dot(whole.T, whole, precision=lax.Precision.HIGHEST), "rows")
         share_rows = whole.shape[0] // lax.axis_size("cols")
         owned = lax.dynamic_slice_in_dim(whole, lax.axis_index("cols") * share_rows, share_rows, 0)

time: 600 us -> 580 us (0.967)
  waiting for transfers between devices: 362 us -> 343 us
    psum x2 -> x0, waiting for transfers between devices: 219 us -> none  [shards(): whole = lax.psum(partial_value, 'cols')]
    all_gather x0 -> x2, waiting for transfers between devices: none -> 202 us  [shards(): blocks = lax.all_gather(partial_value, 'cols')]
where the time goes in v1:
time: 580 us; the launch traced here: 578 us
  waiting for transfers between devices  343 us (59%)
  other arithmetic  117 us (20%)
  blocking collectives  65.7 us (11%)
  local copies, waits for them, and re-layouts  18.6 us (3%)
  between operations  17.4 us (3%)
  matrix products  16 us (3%)
    all_gather x2, waiting for transfers between devices, shards(): blocks = lax.all_gather(partial_value, 'cols')  202 us
    psum x2, waiting for transfers between devices, shards(): lax.psum(jnp.dot(whole.T, whole, precision=lax.Precision.HIGHEST), 'rows')  141 us
    all_gather x2, blocking collectives, shards(): gathered = lax.all_gather(current, 'rows', axis=0, tiled=True)  65.7 us
    another operation x14, other arithmetic, shards(): factor = jnp.linalg.cholesky(gram_matrix)  51.6 us
    another operation x11, other arithmetic, shards(): lax.linalg.triangular_solve(factor, owned, left_side=False, lower=True, t...  40.9 us
    gather x4, local copies, waits for them, and re-layouts, one_block(): picked = jnp.take(tile_stack, colids, axis=0)  13 us
    scatter-add x4, other arithmetic, one_block(): return running.at[rowids].add(products * live_mask[:, None, None])  11.9 us
  transfers between devices with their start and end apart: 4, of which 4 were waited for; matrix products, arithmetic and copies ran while one was open for 0% of the time, Pallas kernels for 0%

profile of v1, /device:TPU:0, one launch (start us, length us, event | category | flops | bytes accessed | tf_op | source)
XLA Modules:
  0.0 578.4 jit_solution(5261142103797223321)
XLA Ops:
  7.9 0.7 reduce.8
  8.6 0.7 reduce.9
  9.3 33.6 %all_gather.12 = bf16[2048,160]{0,1:T(8,128)(2,1)S(1)} all-gather(bf16[256,160]{0,1:T(8,128)(2,1)} %param.18), channel_id=1, replica_groups=mesh['rows'=8,'cols'=4] {'rows'}, dimensions={0}, use_global_device_ids=true | all-gather | bytes 737280 | tf_op jit(solution)/shard_map/all_gather | solution.py:48
  42.9 1.3 copy.27
  44.2 19.8 %while.23 = (s32[]{:T(128)}, f32[8,128,160]{1,2,0:T(8,128)S(1)}, s32[]{:T(128)}, s32[320]{0:T(512)S(1)}, bf16[320,128,128]{2,1,0:T(8,128)(2,1)}, /*index=5*/s32[...) while((s32[]{:T(128)}, f32[8,128,160]{1,2,0:T(8,128)S(1)}, ...), condition=%wide.region_2.4_spmd, body=%wide.region_0.3_spmd.sunk | while | flops 169739648 | bytes 16258423 | solution.py:34
  44.3 0.7 compare_and_fusion.4
  45.0 3.3 gather_fusion
  48.3 2.8 fusion.67
  51.1 3.0 scatter_fusion
  54.1 0.7 compare_and_fusion.4
  54.9 3.3 gather_fusion
  58.1 2.8 fusion.67
  61.0 3.0 scatter_fusion
  64.4 0.9 all_gather_reshape.6
  65.5 102.1 %all-gather.3.cloned.1.call-done = f32[4,1024,160]{1,2,0:T(8,128)} async-done(((f32[1,1024,160]{1,2,0:T(8,128)}), f32[4,1024,160]{1,2,0:T(8,128)}) %all-gather.3.cloned.1.call-update) | async-done | bytes 2621456 | tf_op jit(solution)/shard_map/all_gather | solution.py:50
  167.6 2.0 reduce_sum.18
  169.6 1.4 fusion.45
  171.2 70.3 %all-reduce.6.cloned.1.call-done = f32[160,160]{0,1:T(8,128)} async-done(((f32[160,160]{0,1:T(8,128)}), f32[160,160]{0,1:T(8,128)}) %all-reduce.6.cloned.1.call-update) | async-done | bytes 102416 | tf_op jit(solution)/shard_map/psum | solution.py:52
  241.5 0.9 broadcast_multiply_fusion.1
  242.5 0.9 fusion.21
  243.5 11.7 %cholesky.136 = f32[128,128]{1,0:T(8,128)S(1)} custom-call(f32[128,128]{1,0:T(8,128)S(1)} %cholesky.208), custom_call_target="Cholesky" | custom-call | tf_op jit(solution)/shard_map/jit(cholesky)/cholesky | solution.py:56
  255.2 9.8 %custom-call.13 = f32[1,128,128]{1,2,0:T(8,128)S(1)} custom-call(f32[1,128,128]{2,1,0:T(8,128)S(1)} %get-tuple-element.186), custom_call_target="InvertDiagBlocksLowerTriangular" | custom-call | tf_op jit(solution)/shard_map/jit(cholesky)/cholesky | solution.py:56
  265.4 2.9 cholesky.156
  268.3 0.7 compare_reduce_fusion.2
  271.2 19.7 %custom-call.14 = f32[2,128,128]{1,2,0:T(8,128)S(1)} custom-call(f32[2,128,128]{2,1,0:T(8,128)S(1)} %pad_maximum_fusion.1), custom_call_target="InvertDiagBlocksLowerTriangular" | custom-call | tf_op jit(solution)/shard_map/triangular_solve/custom-call.0 | solution.py:57
  291.6 32.0 %all_gather.14 = bf16[2048,160]{0,1:T(8,128)(2,1)S(1)} all-gather(bf16[256,160]{0,1:T(8,128)(2,1)S(1)} %maximum_convert_fusion), channel_id=1, replica_groups=mesh['rows'=8,'cols'=4] {'rows'}, dimensions={0}, use_global_device_ids=true | all-gather | bytes 737280 | tf_op jit(solution)/shard_map/all_gather | solution.py:48
  323.7 1.3 copy.39
  325.0 19.8 %while.24 = (s32[]{:T(128)}, f32[8,128,160]{1,2,0:T(8,128)S(1)}, s32[]{:T(128)}, s32[320]{0:T(512)S(1)}, bf16[320,128,128]{2,1,0:T(8,128)(2,1)}, /*index=5*/s32[...) while((s32[]{:T(128)}, f32[8,128,160]{1,2,0:T(8,128)S(1)}, ...), condition=%wide.region_11.15_spmd, body=%wide.region_9.14_spmd.sunk | while | flops 169739648 | bytes 16258423 | solution.py:34
  325.0 0.7 compare_and_fusion.5
  325.8 3.3 gather_fusion.1
  329.0 2.8 fusion.70
  331.9 3.0 scatter_fusion.1
  334.9 0.7 compare_and_fusion.5
  335.7 3.3 gather_fusion.1
  338.9 2.8 fusion.70
  341.8 3.0 scatter_fusion.1
  345.2 0.9 all_gather_reshape.7
  346.4 100.3 %all-gather.5.cloned.1.call-done = f32[4,1024,160]{1,2,0:T(8,128)} async-done(((f32[1,1024,160]{1,2,0:T(8,128)}), f32[4,1024,160]{1,2,0:T(8,128)}) %all-gather.5.cloned.1.call-update) | async-done | bytes 2621456 | tf_op jit(solution)/shard_map/all_gather | solution.py:50
  446.7 2.0 reduce_sum.19
  448.7 1.4 fusion.46
  450.1 70.4 %all-reduce.8.cloned.1.call-done = f32[160,160]{0,1:T(8,128)} async-done(((f32[160,160]{0,1:T(8,128)}), f32[160,160]{0,1:T(8,128)}) %all-reduce.8.cloned.1.call-update) | async-done | bytes 102416 | tf_op jit(solution)/shard_map/psum | solution.py:52
  520.5 0.9 broadcast_multiply_fusion
  521.6 0.9 fusion.20
  522.5 11.7 %cholesky.174 = f32[128,128]{1,0:T(8,128)S(1)} custom-call(f32[128,128]{1,0:T(8,128)S(1)} %cholesky.211), custom_call_target="Cholesky" | custom-call | tf_op jit(solution)/shard_map/jit(cholesky)/cholesky | solution.py:56
  534.3 9.8 %custom-call.15 = f32[1,128,128]{1,2,0:T(8,128)S(1)} custom-call(f32[1,128,128]{2,1,0:T(8,128)S(1)} %get-tuple-element.184), custom_call_target="InvertDiagBlocksLowerTriangular" | custom-call | tf_op jit(solution)/shard_map/jit(cholesky)/cholesky | solution.py:56
  544.4 2.9 cholesky.194
  550.0 0.7 fusion.23
  550.8 19.7 %custom-call.16 = f32[2,128,128]{1,2,0:T(8,128)S(1)} custom-call(f32[2,128,128]{2,1,0:T(8,128)S(1)} %pad_maximum_fusion.2), custom_call_target="InvertDiagBlocksLowerTriangular" | custom-call | tf_op jit(solution)/shard_map/triangular_solve/custom-call.0 | solution.py:57
  (55 shorter events, 7.1 us)
Async XLA Ops:
  7.2 160.4 %all-gather.3.cloned.1.call-start = ((), (), s32[]{:S(2)}) async-start(), calls=%async_computation | async-start | bytes 3276800 | tf_op jit(solution)/shard_map/all_gather | solution.py:50
  65.4 176.1 %all-reduce.6.cloned.1.call-start = ((), (), s32[]{:S(2)}) async-start(), calls=%async_computation.1 | async-start | bytes 327680 | tf_op jit(solution)/shard_map/psum | solution.py:52
  171.0 275.7 %all-gather.5.cloned.1.call-start = ((), (), s32[]{:S(2)}) async-start(), calls=%async_computation.2 | async-start | bytes 3276800 | tf_op jit(solution)/shard_map/all_gather | solution.py:50
  346.2 174.3 %all-reduce.8.cloned.1.call-start = ((), (), s32[]{:S(2)}) async-start(), calls=%async_computation.3 | async-start | bytes 327680 | tf_op jit(solution)/shard_map/psum | solution.py:52
Sparse Core Ops, SparseCore 0:
  65.5 102.0 all-gather.2
  171.5 69.9 all-reduce.5
  346.3 100.3 all-gather.4
  450.5 69.9 all-reduce.7

commit v2 on v0

--- a/solution.py
+++ b/solution.py
@@ -48,7 +48,9 @@
         gathered = lax.all_gather(current, "rows", axis=0, tiled=True)
         partial_value = accumulate(own_values, own_rows, own_cols, own_count, gathered, RT)
         whole = lax.psum(partial_value, "cols")
-        gram_matrix = lax.psum(jnp.dot(whole.T, whole, precision=lax.Precision.HIGHEST), "rows")
+        part = jnp.dot(whole.T, whole, precision=lax.Precision.HIGHEST)
+        parts = lax.all_gather(part, "rows", axis=0, tiled=False)
+        gram_matrix = parts.sum(axis=0)
         share_rows = whole.shape[0] // lax.axis_size("cols")
         owned = lax.dynamic_slice_in_dim(whole, lax.axis_index("cols") * share_rows, share_rows, 0)
         gram_matrix = gram_matrix / nodes_total

time: 600 us -> 523 us (0.87)
  waiting for transfers between devices: 362 us -> 220 us
  blocking collectives: 65.7 us -> 135 us
    psum x2 -> x0, waiting for transfers between devices: 142 us -> none  [shards(): lax.psum(jnp.dot(whole.T, whole, precision=lax.Precision.HIGHEST), 'rows')]
    all_gather x0 -> x2, blocking collectives: none -> 69.4 us  [shards(): parts = lax.all_gather(part, 'rows', axis=0, tiled=False)]
  transfers between devices with their start and end apart: 4 -> 2, of which waited for: 4 -> 2; matrix products, arithmetic and copies ran while one was open for 0% -> 0% of each run, Pallas kernels for 0% -> 0%
where the time goes in v2:
time: 523 us; the launch traced here: 521 us
  waiting for transfers between devices  220 us (42%)
  blocking collectives  135 us (26%)
  other arithmetic  109 us (21%)
  matrix products  20.6 us (4%)
  local copies, waits for them, and re-layouts  18 us (3%)
  between operations  17.6 us (3%)
    psum x2, waiting for transfers between devices, shards(): whole = lax.psum(partial_value, 'cols')  220 us
    all_gather x2, blocking collectives, shards(): parts = lax.all_gather(part, 'rows', axis=0, tiled=False)  69.4 us
    all_gather x2, blocking collectives, shards(): gathered = lax.all_gather(current, 'rows', axis=0, tiled=True)  65.4 us
    another operation x14, other arithmetic, shards(): factor = jnp.linalg.cholesky(gram_matrix)  51.6 us
    another operation x11, other arithmetic, shards(): lax.linalg.triangular_solve(factor, owned, left_side=False, lower=True, t...  40.9 us
    gather x4, local copies, waits for them, and re-layouts, one_block(): picked = jnp.take(tile_stack, colids, axis=0)  13 us
    scatter-add x4, other arithmetic, one_block(): return running.at[rowids].add(products * live_mask[:, None, None])  11.9 us
    dot_general x4, matrix products, one_block(): jnp.einsum('sab,sbk->sak', block_values, picked, preferred_element_type=j...  11.2 us
  transfers between devices with their start and end apart: 2, of which 2 were waited for; matrix products, arithmetic and copies ran while one was open for 0% of the time, Pallas kernels for 0%

profile of v2, /device:TPU:0, one launch (start us, length us, event | category | flops | bytes accessed | tf_op | source)
XLA Modules:
  0.0 521.0 jit_solution(1084597358462860088)
XLA Ops:
  7.9 0.7 reduce.8
  8.6 0.7 reduce.9
  9.3 33.6 %all_gather.18 = bf16[2048,160]{0,1:T(8,128)(2,1)S(1)} all-gather(bf16[256,160]{0,1:T(8,128)(2,1)} %param.18), channel_id=1, replica_groups=mesh['rows'=8,'cols'=4] {'rows'}, dimensions={0}, use_global_device_ids=true | all-gather | bytes 737280 | tf_op jit(solution)/shard_map/all_gather | solution.py:48
  42.9 1.3 copy.23
  44.2 19.8 %while.23 = (s32[]{:T(128)}, f32[8,128,160]{1,2,0:T(8,128)S(1)}, s32[]{:T(128)}, s32[320]{0:T(512)S(1)}, bf16[320,128,128]{2,1,0:T(8,128)(2,1)}, /*index=5*/s32[...) while((s32[]{:T(128)}, f32[8,128,160]{1,2,0:T(8,128)S(1)}, ...), condition=%wide.region_2.4_spmd, body=%wide.region_0.3_spmd.sunk | while | flops 169739648 | bytes 16258423 | solution.py:34
  44.3 0.7 compare_and_fusion.4
  45.0 3.3 gather_fusion
  48.3 2.8 fusion.69
  51.1 3.0 scatter_fusion
  54.1 0.7 compare_and_fusion.4
  54.9 3.3 gather_fusion
  58.1 2.8 fusion.69
  61.0 3.0 scatter_fusion
  64.0 0.9 copy_bitcast_fusion.1
  65.1 110.6 %all-reduce.6.cloned.1.call-done = f32[1024,160]{0,1:T(8,128)} async-done(((f32[1024,160]{0,1:T(8,128)}), f32[1024,160]{0,1:T(8,128)}) %all-reduce.6.cloned.1.call-update) | async-done | bytes 655376 | tf_op jit(solution)/shard_map/psum | solution.py:50
  175.6 2.0 fusion.45
  177.6 34.8 %all-gather = f32[1280,160]{1,0:T(8,128)S(1)} all-gather(f32[160,160]{1,0:T(8,128)S(1)} %fusion.45), channel_id=2, replica_groups=mesh['rows'=8,'cols'=4] {'rows'}, dimensions={0}, use_global_device_ids=true | all-gather | bytes 921600 | tf_op jit(solution)/shard_map/all_gather | solution.py:52
  212.8 11.7 %cholesky.136 = f32[128,128]{1,0:T(8,128)S(1)} custom-call(f32[128,128]{1,0:T(8,128)S(1)} %cholesky.208), custom_call_target="Cholesky" | custom-call | tf_op jit(solution)/shard_map/jit(cholesky)/cholesky | solution.py:57
  224.5 9.8 %custom-call.13 = f32[1,128,128]{1,2,0:T(8,128)S(1)} custom-call(f32[1,128,128]{2,1,0:T(8,128)S(1)} %get-tuple-element.186), custom_call_target="InvertDiagBlocksLowerTriangular" | custom-call | tf_op jit(solution)/shard_map/jit(cholesky)/cholesky | solution.py:57
  234.7 2.9 cholesky.156
  237.6 0.7 compare_reduce_fusion.2
  238.3 0.6 compare_reduce_fusion.3
  240.4 19.7 %custom-call.14 = f32[2,128,128]{1,2,0:T(8,128)S(1)} custom-call(f32[2,128,128]{2,1,0:T(8,128)S(1)} %pad_maximum_fusion.1), custom_call_target="InvertDiagBlocksLowerTriangular" | custom-call | tf_op jit(solution)/shard_map/triangular_solve/custom-call.0 | solution.py:58
  260.1 1.2 fusion.26
  261.3 1.0 convolution_subtract_fusion.1
  262.5 31.7 %all_gather.21 = bf16[2048,160]{0,1:T(8,128)(2,1)S(1)} all-gather(bf16[256,160]{0,1:T(8,128)(2,1)S(1)} %maximum_convert_fusion), channel_id=1, replica_groups=mesh['rows'=8,'cols'=4] {'rows'}, dimensions={0}, use_global_device_ids=true | all-gather | bytes 737280 | tf_op jit(solution)/shard_map/all_gather | solution.py:48
  294.2 1.3 copy.33
  295.6 20.0 %while.24 = (s32[]{:T(128)}, f32[8,128,160]{1,2,0:T(8,128)S(1)}, s32[]{:T(128)}, s32[320]{0:T(512)S(1)}, bf16[320,128,128]{2,1,0:T(8,128)(2,1)}, /*index=5*/s32[...) while((s32[]{:T(128)}, f32[8,128,160]{1,2,0:T(8,128)S(1)}, ...), condition=%wide.region_11.15_spmd, body=%wide.region_9.14_spmd.sunk | while | flops 169739648 | bytes 16258423 | solution.py:34
  295.8 0.7 compare_and_fusion.5
  296.6 3.3 gather_fusion.1
  299.8 2.8 fusion.72
  302.7 3.0 scatter_fusion.1
  305.7 0.7 compare_and_fusion.5
  306.4 3.3 gather_fusion.1
  309.7 2.8 fusion.72
  312.6 3.0 scatter_fusion.1
  315.6 0.9 copy_bitcast_fusion
  316.5 109.6 %all-reduce.8.cloned.1.call-done = f32[1024,160]{0,1:T(8,128)} async-done(((f32[1024,160]{0,1:T(8,128)}), f32[1024,160]{0,1:T(8,128)}) %all-reduce.8.cloned.1.call-update) | async-done | bytes 655376 | tf_op jit(solution)/shard_map/psum | solution.py:50
  426.1 2.0 fusion.46
  428.1 34.6 %all-gather.1 = f32[1280,160]{1,0:T(8,128)S(1)} all-gather(f32[160,160]{1,0:T(8,128)S(1)} %fusion.46), channel_id=3, replica_groups=mesh['rows'=8,'cols'=4] {'rows'}, dimensions={0}, use_global_device_ids=true | all-gather | bytes 921600 | tf_op jit(solution)/shard_map/all_gather | solution.py:52
  463.1 11.7 %cholesky.174 = f32[128,128]{1,0:T(8,128)S(1)} custom-call(f32[128,128]{1,0:T(8,128)S(1)} %cholesky.211), custom_call_target="Cholesky" | custom-call | tf_op jit(solution)/shard_map/jit(cholesky)/cholesky | solution.py:57
  474.9 9.8 %custom-call.15 = f32[1,128,128]{1,2,0:T(8,128)S(1)} custom-call(f32[1,128,128]{2,1,0:T(8,128)S(1)} %get-tuple-element.184), custom_call_target="InvertDiagBlocksLowerTriangular" | custom-call | tf_op jit(solution)/shard_map/jit(cholesky)/cholesky | solution.py:57
  485.0 2.9 cholesky.194
  490.6 0.7 fusion.23
  491.4 19.7 %custom-call.16 = f32[2,128,128]{1,2,0:T(8,128)S(1)} custom-call(f32[2,128,128]{2,1,0:T(8,128)S(1)} %pad_maximum_fusion.2), custom_call_target="InvertDiagBlocksLowerTriangular" | custom-call | tf_op jit(solution)/shard_map/triangular_solve/custom-call.0 | solution.py:58
  511.0 1.2 fusion.24
  512.3 1.0 convolution_subtract_fusion
  513.5 0.7 pad_maximum_fusion
  (51 shorter events, 4.0 us)
Async XLA Ops:
  7.2 168.5 %all-reduce.6.cloned.1.call-start = ((), (), s32[]{:S(2)}) async-start(), calls=%async_computation | async-start | bytes 1310720 | tf_op jit(solution)/shard_map/psum | solution.py:50
  65.0 361.2 %all-reduce.8.cloned.1.call-start = ((), (), s32[]{:S(2)}) async-start(), calls=%async_computation.1 | async-start | bytes 1310720 | tf_op jit(solution)/shard_map/psum | solution.py:50
Sparse Core Ops, SparseCore 0:
  65.1 110.4 all-reduce.5
  316.7 109.4 all-reduce.7
